TPU v7x, 32 devices: a whole 2x2x4 slice. The times are simulated.
32 devices in a mesh: ep: 16 (over z, y, x), tp: 2 (over core).
Axes of the slice: x: 2, y: 2, z: 4, core: 2. Of those that a mesh axis runs over, the one named last changes fastest.
Arguments:
- tokens: bfloat16 [256, 7168], P('ep', 'tp'), may hold values from -6 to 6
- route_ids: int32 [256, 8], P('ep'), may hold values from 0 to 15, all different within a row; in each aligned block of 16 rows (0 to 15, 16 to 31, ...) at most 16 rows name the same one
- expert_slot: int32 [16], replicated, may hold values from 0 to 15, each once
- router_weight: bfloat16 [7168, 16], P('tp'), may hold values from -0.0625 to 0.0625
- expert_gate: bfloat16 [16, 7168, 1024], P('ep', 'tp'), may hold values from -0.0625 to 0.0625
- expert_up: bfloat16 [16, 7168, 1024], P('ep', 'tp'), may hold values from -0.0625 to 0.0625
- expert_down: bfloat16 [16, 1024, 7168], P('ep', None, 'tp'), may hold values from -0.1875 to 0.1875
- shared_gate: bfloat16 [7168, 1024], P('tp', 'ep'), may hold values from -0.0625 to 0.0625
- shared_up: bfloat16 [7168, 1024], P('tp', 'ep'), may hold values from -0.0625 to 0.0625
- shared_down: bfloat16 [1024, 7168], P('ep', 'tp'), may hold values from -0.1875 to 0.1875
Outputs:
- mixed: bfloat16 [256, 7168], P('ep', 'tp')
Inputs may be any that keep to these rules, and one draw needn't show every extreme that they name: `route_ids`: each row names 8 different experts. Among the rows of one device (the aligned blocks of 16 rows) no expert is named more than 16 times, and in some blocks one expert is named exactly 16 times. A permutation of 0 to 15; the weights of expert e lie in row expert_slot[e] of the expert weight arrays.
All inputs are finite; a program needn't handle non-finite values.
Results may differ from a plain program's by a relative error of at most 0.003.
Values may be sent and summed in bfloat16 or wider, within the bound.
A program may use at most 128 MiB of HBM per device.

v0:
```python
import jax
import jax.numpy as jnp
from jax import lax
from jax.sharding import PartitionSpec as P

route_scale = 2.5


def taken_in(piece, axis, dim):

    def gathered(part):
        return lax.all_gather(part, axis, axis=dim, tiled=True)

    return jax.tree.map(gathered, piece)


def shared_ffn(pre_gate, pre_up, shared_down):
    hidden = (jax.nn.silu(pre_gate) * pre_up).astype(jnp.bfloat16)

    def add_rows(total, piece):
        columns = lax.slice_in_dim(hidden, 0, piece.shape[0], axis=1)
        return total + jnp.dot(columns, piece, preferred_element_type=jnp.float32)

    empty = jnp.zeros((hidden.shape[0], shared_down.shape[1]), jnp.float32)
    return add_rows(empty, taken_in(shared_down, "ep", 0))


def on_device(
    tokens,
    route_ids,
    expert_slot,
    router_weight,
    expert_gate,
    expert_up,
    expert_down,
    shared_gate,
    shared_up,
    shared_down,
):
    tok_rows = tokens.shape[0]
    features = tokens.shape[1]
    top_count = route_ids.shape[1]
    experts_all = expert_slot.shape[0]
    local_count = expert_gate.shape[0]
    capacity = max(2, 2 * tok_rows * top_count // experts_all)
    groups = lax.axis_size("ep")
    shared_width = shared_gate.shape[1] * groups
    part_logits = jnp.dot(tokens, router_weight, preferred_element_type=jnp.float32)

    def add_columns(totals, pieces, start):
        gate_piece = jnp.dot(tokens, pieces[0], preferred_element_type=jnp.float32)
        up_piece = jnp.dot(tokens, pieces[1], preferred_element_type=jnp.float32)
        gate_total = lax.dynamic_update_slice_in_dim(totals[0], gate_piece, start, 1)
        up_total = lax.dynamic_update_slice_in_dim(totals[1], up_piece, start, 1)
        return (gate_total, up_total)

    blank = jnp.zeros((tok_rows, shared_width), jnp.float32)
    part_gate, part_up = add_columns(
        (blank, blank), taken_in((shared_gate, shared_up), "ep", 1), jnp.int32(0)
    )
    logits = lax.psum(part_logits, "tp")
    shared_pre_gate, shared_pre_up = lax.psum((part_gate, part_up), "tp")
    scores = jax.nn.sigmoid(logits)
    picked = jnp.take_along_axis(scores, route_ids, axis=1)
    gate_values = picked / jnp.sum(picked, axis=1, keepdims=True) * route_scale
    flat_ids = route_ids.reshape(-1)
    onehot = (flat_ids[:, None] == jnp.arange(experts_all, dtype=jnp.int32)[None, :]).astype(
        jnp.int32
    )
    earlier = jnp.cumsum(onehot, axis=0) - onehot
    places = jnp.take_along_axis(earlier, flat_ids[:, None], axis=1)[:, 0]
    target_rows = expert_slot[flat_ids] * capacity + places
    owners = jnp.arange(flat_ids.shape[0], dtype=jnp.int32) // top_count
    outgoing = (
        jnp.zeros((experts_all * capacity, features), tokens.dtype)
        .at[target_rows]
        .set(tokens[owners])
    )
    arrived = lax.all_to_all(outgoing, "ep", split_axis=0, concat_axis=0, tiled=True)
    grouped = arrived.reshape(groups, local_count, capacity, features).transpose(1, 0, 2, 3)
    grouped = grouped.reshape(local_count, groups * capacity, features)
    pre_gate = jnp.einsum("erd,edf->erf", grouped, expert_gate, preferred_element_type=jnp.float32)
    pre_up = jnp.einsum("erd,edf->erf", grouped, expert_up, preferred_element_type=jnp.float32)
    pre_gate, pre_up = lax.psum((pre_gate, pre_up), "tp")
    hidden = (jax.nn.silu(pre_gate) * pre_up).astype(jnp.bfloat16)
    produced = jnp.einsum(
        "erf,efd->erd", hidden, expert_down, preferred_element_type=jnp.float32
    ).astype(jnp.bfloat16)
    leaving = produced.reshape(local_count, groups, capacity, features).transpose(1, 0, 2, 3)
    leaving = leaving.reshape(groups * local_count * capacity, features)
    returned = lax.all_to_all(leaving, "ep", split_axis=0, concat_axis=0, tiled=True)
    weighted = returned[target_rows].astype(jnp.float32) * gate_values.reshape(-1)[:, None]
    routed = jnp.sum(weighted.reshape(tok_rows, top_count, features), axis=1)
    shared_out = shared_ffn(shared_pre_gate, shared_pre_up, shared_down)
    return (shared_out + routed).astype(jnp.bfloat16)


def solution(mesh):
    placed = (
        P("ep", "tp"),
        P("ep", None),
        P(),
        P("tp", None),
        P("ep", "tp", None),
        P("ep", "tp", None),
        P("ep", None, "tp"),
        P("tp", "ep"),
        P("tp", "ep"),
        P("ep", "tp"),
    )
    return jax.shard_map(
        on_device, mesh=mesh, in_specs=placed, out_specs=P("ep", "tp"), check_vma=False
    )
```

profile of v0, /device:TPU:0, one launch (start us, length us, event | category | flops | bytes accessed | tf_op | source)
XLA Modules:
  0.0 420.3 jit_solution(3200290772862545923)
XLA Ops:
  6.5 0.7 all-gather.4.cloned.1.call-update
  7.3 0.7 all-gather.6.cloned.1.call-update
  8.1 0.8 copy.17
  9.5 1.3 gather_fusion.1
  10.8 2.0 fusion.33
  12.7 10.2 %fusion.29 = s32[128]{0:T(128)S(1)} fusion(s32[128]{0:T(128)S(1)} %gather_fusion.1, s32[128,1]{0,1:T(1,128)S(1)} %reshape.270, s32[]{:T(128)} %bitcast.18, s32[]{:T(128)} %bitcast.19, s32[]{:T(128)} %bitcast.20, s32[]{:T(128)} %bitcast.21, s32[]{:T(128)} %bitcast.22, s32[]{:T(128)} %bitcast.24, s32[]{:T(128)} %bitcast.23, s32[]{:T(128)} %bitcast.1, ...), kind=kLoop, calls=%fused_computation.65 | loop fusion | flops 5376 | bytes 1600 | tf_op jit(solution)/shard_map/select_n | solution.py:77
  23.0 5.2 %scatter_custom_fusion = bf16[256,3584]{1,0:T(8,128)(2,1)S(1)} fusion(s32[128]{0:T(128)S(1)} %fusion.29, bf16[16,3584]{1,0:T(8,128)(2,1)S(1)} %copy-done, s32[1024]{0:T(1024)S(1)} %pad_clamp_fusion.1, bf16[]{:T(256)} %constant.52.clone.1), kind=kCustom, calls=%fused_computation.19 | custom fusion | bytes 1835010 | tf_op jit(solution)/shard_map/scatter | solution.py:77
  28.2 71.7 %all_to_all.21 = bf16[16,16,3584]{2,1,0:T(8,128)(2,1)S(1)} all-to-all(bf16[16,16,3584]{2,1,0:T(8,128)(2,1)S(1)} %bitcast.195), channel_id=1, replica_groups=mesh['ep'=16,'tp'=2] {'ep'}, dimensions={0} | all-to-all | bytes 3670016 | tf_op jit(solution)/shard_map/all_to_all | solution.py:79
  99.9 6.3 %fusion.11 = f32[1,256,1024]{2,1,0:T(8,128)} fusion(bf16[256,3584]{1,0:T(8,128)(2,1)S(1)} %bitcast.197, bf16[1,3584,1024]{2,1,0:T(8,128)(2,1)} %param.14), kind=kOutput, calls=%fused_computation.16 | convolution fusion | flops 1879048192 | bytes 10223616 | tf_op jit(solution)/shard_map/erd,edf->erf/dot_general | solution.py:82
  106.2 3.0 fusion.14
  109.2 32.3 %all-gather.4.cloned.1.call-done = bf16[3584,1024]{0,1:T(8,128)(2,1)} async-done(((bf16[3584,64]{0,1:T(8,128)(2,1)}), bf16[3584,1024]{0,1:T(8,128)(2,1)}) %all-gather.4.cloned.1.call-update) | async-done | bytes 7340048 | tf_op jit(solution)/shard_map/all_gather | solution.py:12
  141.6 5.7 %fusion.34 = f32[16,1024]{1,0:T(8,128)} fusion(bf16[16,3584]{1,0:T(8,128)(2,1)S(1)} %copy-done, bf16[3584,1024]{0,1:T(8,128)(2,1)} %all-gather.4.cloned.1.call-done), kind=kOutput, calls=%fused_computation.71 | convolution fusion | flops 117440512 | bytes 7520256 | tf_op jit(solution)/shard_map/dot_general | solution.py:51
  147.3 98.3 %all-gather.6.cloned.1.call-done = bf16[3584,1024]{0,1:T(8,128)(2,1)} async-done(((bf16[3584,64]{0,1:T(8,128)(2,1)}), bf16[3584,1024]{0,1:T(8,128)(2,1)}) %all-gather.6.cloned.1.call-update) | async-done | bytes 7340048 | tf_op jit(solution)/shard_map/all_gather | solution.py:12
  245.5 5.7 %fusion.35 = f32[16,1024]{1,0:T(8,128)} fusion(bf16[16,3584]{1,0:T(8,128)(2,1)S(1)} %copy-done, bf16[3584,1024]{0,1:T(8,128)(2,1)} %all-gather.6.cloned.1.call-done), kind=kOutput, calls=%fused_computation.72 | convolution fusion | flops 117440512 | bytes 7520256 | tf_op jit(solution)/shard_map/dot_general | solution.py:52
  251.9 19.4 %all-reduce.3.cloned.1.call-done = (f32[1,256,1024]{2,1,0:T(8,128)}, f32[1,256,1024]{2,1,0:T(8,128)}, f32[16,1024]{1,0:T(8,128)}, f32[16,1024]{1,0:T(8,128)}) async-done(((f32[1,256,1024]{2,1,0:T(8,128)}, f32[1,256,1024]{2,1,0:T(8,128)}, f32[16,1024]{1,0:T(8,128)}, f32[16,1024]{1,0:T(8,128)}), (f32[1,256,1024]{2,1,0:T(8,128)}, f32[1,256,1024]{2,1,0:T(8,128)}, f32[16,1024]{1,0:T(8,128)}, ...) | async-done | bytes 2228240 | tf_op jit(solution)/shard_map/psum | solution.py:84
  271.3 7.2 %fusion.6 = bf16[256,3584]{1,0:T(8,128)(2,1)} fusion(bf16[1,1024,3584]{2,1,0:T(8,128)(2,1)} %param.16, f32[1,256,1024]{2,1,0:T(8,128)} %get-tuple-element.5, f32[1,256,1024]{2,1,0:T(8,128)} %get-tuple-element.6), kind=kOutput, calls=%fused_computation.11 | convolution fusion | flops 1881538560 | bytes 11272192 | tf_op jit(solution)/shard_map/erf,efd->erd/dot_general | solution.py:86
  278.5 6.8 %all-to-all-start.1 = ((bf16[16,16,3584]{2,1,0:T(8,128)(2,1)}), bf16[16,16,3584]{2,1,0:T(8,128)(2,1)S(1)}, u32[]{:S(2)}, u32[]{:S(2)}) async-start(bf16[16,16,3584]{2,1,0:T(8,128)(2,1)} %bitcast.196), calls=%async_computation.1 | async-start | bytes 3670016 | tf_op jit(solution)/shard_map/all_to_all | solution.py:91
  285.6 2.5 psum.39
  288.2 1.3 gather_fusion.2
  289.7 56.7 %all-to-all-done.1 = bf16[16,16,3584]{2,1,0:T(8,128)(2,1)S(1)} async-done(((bf16[16,16,3584]{2,1,0:T(8,128)(2,1)}), bf16[16,16,3584]{2,1,0:T(8,128)(2,1)S(1)}, u32[]{:S(2)}, u32[]{:S(2)}) %all-to-all-start.1) | async-done | bytes 1835040 | tf_op jit(solution)/shard_map/all_to_all | solution.py:91
  346.4 1.1 gather_fusion
  347.5 0.7 fusion.10
  348.2 60.8 %all-gather.8.cloned.1.call-done = bf16[1024,3584]{1,0:T(8,128)(2,1)} async-done(((bf16[64,3584]{1,0:T(8,128)(2,1)}), bf16[1024,3584]{1,0:T(8,128)(2,1)}) %all-gather.8.cloned.1.call-update) | async-done | bytes 7340048 | tf_op jit(solution)/shard_map/all_gather | solution.py:12
  409.0 4.8 %fusion.9 = bf16[16,3584]{1,0:T(8,128)(2,1)} fusion(f32[16,3584]{1,0:T(8,128)S(1)} %fusion.10, bf16[1024,3584]{1,0:T(8,128)(2,1)} %all-gather.8.cloned.1.call-done, f32[16,1024]{1,0:T(8,128)S(1)} %copy-done.2, f32[16,1024]{1,0:T(8,128)S(1)} %copy-done.3), kind=kOutput, calls=%fused_computation.13 | convolution fusion | flops 117653504 | bytes 7815168 | tf_op jit(solution)/shard_map/dot_general | solution.py:22
  (44 shorter events, 1.9 us)
Async XLA Ops:
  6.5 16.4 %copy-start = (bf16[16,3584]{1,0:T(8,128)(2,1)S(1)}, bf16[16,3584]{1,0:T(8,128)(2,1)}, u32[]{:S(2)}) copy-start(bf16[16,3584]{1,0:T(8,128)(2,1)} %param.10) | copy-start | bytes 344068
  6.5 135.0 %all-gather.4.cloned.1.call-start = ((), (), s32[]{:S(2)}) async-start(), calls=%async_computation.2 | async-start | bytes 7798784 | tf_op jit(solution)/shard_map/all_gather | solution.py:12
  7.3 238.3 %all-gather.6.cloned.1.call-start = ((), (), s32[]{:S(2)}) async-start(), calls=%async_computation.3 | async-start | bytes 7798784 | tf_op jit(solution)/shard_map/all_gather | solution.py:12
  8.0 263.3 %all-reduce.3.cloned.1.call-start = ((), (), s32[]{:S(2)}) async-start(), calls=%async_computation.5 | async-start | bytes 4456448 | tf_op jit(solution)/shard_map/psum | solution.py:84
  28.2 78.0 %slice-start = ((s8[7340032]{0:T(1024)(128)(4,1)}), s8[4194304]{0:T(1024)(128)(4,1)S(1)}, s32[]{:S(2)}) async-start(s8[7340032]{0:T(1024)(128)(4,1)} %bitcast.199), calls=%async_computation.6 | async-start | bytes 8388608
  99.9 6.3 %slice-start.1 = ((s8[7340032]{0:T(1024)(128)(4,1)}), s8[3145728]{0:T(1024)(128)(4,1)S(1)}, s32[]{:S(2)}) async-start(s8[7340032]{0:T(1024)(128)(4,1)} %bitcast.199), calls=%async_computation.7 | async-start | bytes 6291456
  251.3 157.7 %all-gather.8.cloned.1.call-start = ((), (), s32[]{:S(2)}) async-start(), calls=%async_computation.4 | async-start | bytes 7798784 | tf_op jit(solution)/shard_map/all_gather | solution.py:12
  271.3 14.0 %copy-start.4 = (s32[16,8]{0,1:T(8,128)S(1)}, s32[16,8]{0,1:T(8,128)}, u32[]{:S(2)}) copy-start(s32[16,8]{0,1:T(8,128)} %param.11) | copy-start | bytes 1540
  271.3 14.2 %copy-start.1 = (bf16[3584,16]{0,1:T(8,128)(2,1)S(1)}, bf16[3584,16]{0,1:T(8,128)(2,1)}, u32[]{:S(2)}) copy-start(bf16[3584,16]{0,1:T(8,128)(2,1)} %param.13) | copy-start | bytes 344068
  278.5 67.9 %all-to-all-start.1 = ((bf16[16,16,3584]{2,1,0:T(8,128)(2,1)}), bf16[16,16,3584]{2,1,0:T(8,128)(2,1)S(1)}, u32[]{:S(2)}, u32[]{:S(2)}) async-start(bf16[16,16,3584]{2,1,0:T(8,128)(2,1)} %bitcast.196), calls=%async_computation.1 | async-start | bytes 3670016 | tf_op jit(solution)/shard_map/all_to_all | solution.py:91
  288.1 120.8 %copy-start.2 = (f32[16,1024]{1,0:T(8,128)S(1)}, f32[16,1024]{1,0:T(8,128)}, u32[]{:S(2)}) copy-start(f32[16,1024]{1,0:T(8,128)} %get-tuple-element.7) | copy-start | bytes 196612
  288.1 120.8 %copy-start.3 = (f32[16,1024]{1,0:T(8,128)S(1)}, f32[16,1024]{1,0:T(8,128)}, u32[]{:S(2)}) copy-start(f32[16,1024]{1,0:T(8,128)} %get-tuple-element.8) | copy-start | bytes 196612
Sparse Core Ops, SparseCore 0:
  10.0 131.5 all-gather.3
  144.3 101.2 all-gather.5
  251.4 19.8 all-reduce.2
  273.8 135.0 all-gather.7
where the time goes:
time: 421 us; the launch traced here: 420 us
  waiting for transfers between devices  269 us (64%)
  blocking collectives  74.2 us (18%)
  matrix products  32.8 us (8%)
  between operations  13.3 us (3%)
  local copies, waits for them, and re-layouts  12.2 us (3%)
  other arithmetic  11.4 us (3%)
  starting transfers between devices  7.14 us (2%)
    all_gather x3, waiting for transfers between devices, gathered(): return lax.all_gather(part, axis, axis=dim, tiled=True)  191 us
    all_to_all x1, blocking collectives, on_device(): lax.all_to_all(outgoing, 'ep', split_axis=0, concat_axis=0, tiled=True)  71.7 us
    all_to_all x1, waiting for transfers between devices, on_device(): lax.all_to_all(leaving, 'ep', split_axis=0, concat_axis=0, tiled=True)  56.7 us
    psum x1, waiting for transfers between devices, on_device(): pre_gate, pre_up = lax.psum((pre_gate, pre_up), 'tp')  19.4 us
    select_n x1, other arithmetic, on_device(): outgoing = jnp.zeros((experts_all * capacity, features), tokens.dtype).at...  10.2 us
  transfers between devices with their start and end apart: 5, of which 5 were waited for; matrix products, arithmetic and copies ran while one was open for 11% of the time, Pallas kernels for 0%

commit v1 on v0

v1 whole, which is shorter than its diff:
```python
import functools

import jax
import jax.numpy as jnp
from jax import lax
from jax.experimental import pallas as pl
from jax.experimental.pallas import tpu as pltpu
from jax.sharding import PartitionSpec as P
import math

route_scale = 2.5
MESH = pl.DeviceIdType.MESH


def silu(v):
    return v / (1.0 + jnp.exp(-v))


def dot(a, b):
    return jnp.dot(a, b, preferred_element_type=jnp.float32)


def kernel(
    n_ep,
    n_tp,
    chunks,
    tokens,
    ids,
    slot,
    rw_hbm,
    eg_hbm,
    eu_hbm,
    ed_hbm,
    sg_hbm,
    su_hbm,
    sd_hbm,
    out,
    x,
    wg,
    wu,
    wd,
    rw,
    sg,
    su,
    sw,
    sd,
    lg_part,
    lg_in,
    gates,
    gates_in,
    part,
    part_in,
    sh_part,
    sh_in,
    hid,
    hid_in,
    leave,
    arrive,
    w_sem,
    own_sem,
    x_send,
    x_recv,
    lg_send,
    lg_recv,
    ga_send,
    ga_recv,
    pa_send,
    pa_recv,
    sh_send,
    sh_recv,
    hi_send,
    hi_recv,
    le_send,
    le_recv,
):
    ep, tp = lax.axis_index("ep"), lax.axis_index("tp")
    rows, feats = tokens.shape
    experts = slot.shape[1]
    ff_part = wg.shape[2]
    sff = sg.shape[1]
    width = feats // chunks

    def ep_at(d):
        return lax.rem(ep + d, n_ep)

    def tp_at(d):
        return lax.rem(tp + d, n_tp)

    def row_block(ref, block):
        return ref.at[pl.ds(pl.multiple_of(block * rows, rows), rows), :]

    loads = [
        pltpu.make_async_copy(rw_hbm, rw, w_sem.at[0]),
        pltpu.make_async_copy(sg_hbm, sg, w_sem.at[1]),
        pltpu.make_async_copy(su_hbm, su, w_sem.at[2]),
        pltpu.make_async_copy(sd_hbm, sd, w_sem.at[3]),
        pltpu.make_async_copy(ed_hbm.at[0], wd, w_sem.at[4]),
    ]

    def piece_load(hbm, buf, j, sem):
        cols = pl.ds(pl.multiple_of(j * ff_part, ff_part), ff_part)
        return pltpu.make_async_copy(hbm.at[0, :, cols], buf.at[j], w_sem.at[sem + j])

    for load in loads[:3]:
        load.start()
    for j in range(n_tp):
        piece_load(eg_hbm, wg, j, 5).start()
        piece_load(eu_hbm, wu, j, 5 + n_tp).start()
    for load in loads[3:]:
        load.start()
    own = pltpu.make_async_copy(tokens, row_block(x, ep), own_sem.at[0])
    own.start()

    barrier = pltpu.get_barrier_semaphore()

    @pl.loop(1, n_ep)
    def _(d):
        pl.semaphore_signal(barrier, inc=1, device_id={"ep": ep_at(d)}, device_id_type=MESH)

    @pl.loop(1, n_tp)
    def _(d):
        pl.semaphore_signal(barrier, inc=1, device_id={"tp": tp_at(d)}, device_id_type=MESH)

    pl.semaphore_wait(barrier, n_ep + n_tp - 2)

    def token_copy(src, to):
        return pltpu.make_async_remote_copy(
            src_ref=tokens,
            dst_ref=row_block(x, src),
            send_sem=x_send.at[to],
            recv_sem=x_recv.at[src],
            device_id={"ep": to},
            device_id_type=MESH,
        )

    @pl.loop(1, n_ep)
    def _(d):
        token_copy(ep, ep_at(d)).start()

    def to_tp(src_ref, in_ref, send, recv, slot_in, to):
        return pltpu.make_async_remote_copy(
            src_ref=src_ref,
            dst_ref=in_ref.at[slot_in],
            send_sem=send.at[to],
            recv_sem=recv.at[slot_in],
            device_id={"tp": to},
            device_id_type=MESH,
        )

    loads[0].wait()
    lg_part[...] = dot(tokens[...], rw[...])
    lg_in[tp] = lg_part[...]

    @pl.loop(1, n_tp)
    def _(d):
        to_tp(lg_part, lg_in, lg_send, lg_recv, tp, tp_at(d)).start()

    loads[1].wait()
    loads[2].wait()
    sw[:, 0:sff] = sg[...]
    sw[:, sff : 2 * sff] = su[...]

    @pl.loop(1, n_tp)
    def _(d):
        to_tp(lg_part, lg_in, lg_send, lg_recv, tp_at(d), tp_at(d)).wait()

    logits = lg_in[0]
    for j in range(1, n_tp):
        logits = logits + lg_in[j]
    expert_iota = lax.broadcasted_iota(jnp.int32, (rows, experts), 1)
    mask = jnp.zeros((rows, experts), jnp.float32)
    for k in range(ids.shape[1]):
        mask = mask + jnp.where(ids[:, k : k + 1] == expert_iota, 1.0, 0.0)
    picked = mask * (1.0 / (1.0 + jnp.exp(-logits)))
    gates[...] = picked / jnp.sum(picked, axis=1, keepdims=True) * route_scale
    gates_in[pl.ds(pl.multiple_of(ep * rows, rows), rows), :] = gates[...]

    def gate_copy(src, to):
        return pltpu.make_async_remote_copy(
            src_ref=gates,
            dst_ref=row_block(gates_in, src),
            send_sem=ga_send.at[to],
            recv_sem=ga_recv.at[src],
            device_id={"ep": to},
            device_id_type=MESH,
        )

    @pl.loop(1, n_ep)
    def _(d):
        gate_copy(ep, ep_at(d)).start()

    own.wait()

    @pl.loop(1, n_ep)
    def _(d):
        token_copy(ep_at(d), ep_at(d)).wait()

    def gate_up(j):
        piece_load(eg_hbm, wg, j, 5).wait()
        piece_load(eu_hbm, wu, j, 5 + n_tp).wait()
        part[j, 0] = dot(x[...], wg[j])
        part[j, 1] = dot(x[...], wu[j])

    @pl.loop(1, n_tp)
    def _(d):
        j = tp_at(d)
        gate_up(j)
        to_tp(part.at[j], part_in, pa_send, pa_recv, tp, j).start()

    sh_part[...] = dot(x[...], sw[...])

    @pl.loop(1, n_tp)
    def _(d):
        to_tp(sh_part, sh_in, sh_send, sh_recv, tp, tp_at(d)).start()

    gate_up(tp)

    @pl.loop(1, n_tp)
    def _(d):
        j = tp_at(d)
        to_tp(part.at[j], part_in, pa_send, pa_recv, j, j).wait()

    @pl.loop(1, n_tp)
    def _(d):
        j = tp_at(d)
        part[tp] = part[tp] + part_in[j]

    hid[...] = (silu(part[tp, 0]) * part[tp, 1]).astype(jnp.bfloat16)
    hid_in[tp] = hid[...]

    @pl.loop(1, n_tp)
    def _(d):
        to_tp(hid, hid_in, hi_send, hi_recv, tp, tp_at(d)).start()

    @pl.loop(1, n_tp)
    def _(d):
        j = tp_at(d)
        to_tp(sh_part, sh_in, sh_send, sh_recv, j, j).wait()

    sh_in[tp] = sh_part[...]
    sh_sum = sh_in[0]
    for j in range(1, n_tp):
        sh_sum = sh_sum + sh_in[j]
    sh_hid = (silu(sh_sum[:, 0:sff]) * sh_sum[:, sff : 2 * sff]).astype(jnp.bfloat16)

    @pl.loop(1, n_ep)
    def _(d):
        gate_copy(ep_at(d), ep_at(d)).wait()

    mine = jnp.where(slot[...] == ep, 1.0, 0.0)
    column = jnp.sum(gates_in[...] * mine, axis=1, keepdims=True)

    loads[3].wait()
    loads[4].wait()

    @pl.loop(1, n_tp)
    def _(d):
        j = tp_at(d)
        to_tp(hid, hid_in, hi_send, hi_recv, j, j).wait()

    def leave_copy(chunk, src, to):
        return pltpu.make_async_remote_copy(
            src_ref=row_block(leave.at[chunk], to),
            dst_ref=row_block(arrive.at[chunk], src),
            send_sem=le_send.at[chunk, to],
            recv_sem=le_recv.at[chunk, src],
            device_id={"ep": to},
            device_id_type=MESH,
        )

    @pl.loop(0, chunks)
    def _(chunk):
        cols = pl.ds(pl.multiple_of(chunk * width, width), width)
        total = dot(hid_in[0], wd[0:ff_part, cols])
        for j in range(1, n_tp):
            total = total + dot(hid_in[j], wd[j * ff_part : (j + 1) * ff_part, cols])
        given = total.astype(jnp.bfloat16).astype(jnp.float32) * column
        given = given + dot(sh_hid, sd[:, cols])
        leave[chunk] = given.astype(jnp.bfloat16)

        @pl.loop(1, n_ep)
        def _(d):
            leave_copy(chunk, ep, ep_at(d)).start()

    @pl.loop(0, chunks)
    def _(chunk):
        cols = pl.ds(pl.multiple_of(chunk * width, width), width)
        here = pl.ds(pl.multiple_of(ep * rows, rows), rows)
        arrive[chunk, here, :] = leave[chunk, here, :]

        @pl.loop(1, n_ep)
        def _(d):
            leave_copy(chunk, ep_at(d), ep_at(d)).wait()

        def add(src, total):
            block = arrive[chunk, pl.ds(pl.multiple_of(src * rows, rows), rows), :]
            return total + block.astype(jnp.float32)

        total = lax.fori_loop(0, n_ep, add, jnp.zeros((rows, width), jnp.float32))
        out[:, cols] = total.astype(jnp.bfloat16)


def on_device(n_ep, n_tp, *args):
    (tokens, ids, slot, rw, eg, eu, ed, sg, su, sd) = args
    rows, feats = tokens.shape
    experts = slot.shape[0]
    ff = eg.shape[2]
    sff = sg.shape[1]
    everyone = rows * n_ep
    ff_part = ff // n_tp
    chunks = math.gcd(feats // 128, 4)
    width = feats // chunks
    bf, f32 = jnp.bfloat16, jnp.float32
    dma = pltpu.SemaphoreType.DMA
    vmem = pl.BlockSpec(memory_space=pltpu.VMEM)
    hbm = pl.BlockSpec(memory_space=pl.ANY)
    return pl.pallas_call(
        functools.partial(kernel, n_ep, n_tp, chunks),
        out_shape=jax.ShapeDtypeStruct((rows, feats), bf),
        in_specs=[vmem] * 3 + [hbm] * 7,
        out_specs=vmem,
        scratch_shapes=[
            pltpu.VMEM((everyone, feats), bf),
            pltpu.VMEM((n_tp, feats, ff_part), bf),
            pltpu.VMEM((n_tp, feats, ff_part), bf),
            pltpu.VMEM((ff, feats), bf),
            pltpu.VMEM((feats, experts), bf),
            pltpu.VMEM((feats, sff), bf),
            pltpu.VMEM((feats, sff), bf),
            pltpu.VMEM((feats, 2 * sff), bf),
            pltpu.VMEM((sff, feats), bf),
            pltpu.VMEM((rows, experts), f32),
            pltpu.VMEM((n_tp, rows, experts), f32),
            pltpu.VMEM((rows, experts), f32),
            pltpu.VMEM((everyone, experts), f32),
            pltpu.VMEM((n_tp, 2, everyone, ff_part), f32),
            pltpu.VMEM((n_tp, 2, everyone, ff_part), f32),
            pltpu.VMEM((everyone, 2 * sff), f32),
            pltpu.VMEM((n_tp, everyone, 2 * sff), f32),
            pltpu.VMEM((everyone, ff_part), bf),
            pltpu.VMEM((n_tp, everyone, ff_part), bf),
            pltpu.VMEM((chunks, everyone, width), bf),
            pltpu.VMEM((chunks, everyone, width), bf),
            dma((5 + 2 * n_tp,)),
            dma((1,)),
            dma((n_ep,)),
            dma((n_ep,)),
            dma((n_tp,)),
            dma((n_tp,)),
            dma((n_ep,)),
            dma((n_ep,)),
            dma((n_tp,)),
            dma((n_tp,)),
            dma((n_tp,)),
            dma((n_tp,)),
            dma((n_tp,)),
            dma((n_tp,)),
            dma((chunks, n_ep)),
            dma((chunks, n_ep)),
        ],
        compiler_params=pltpu.CompilerParams(
            collective_id=0, has_side_effects=True, vmem_limit_bytes=63 * 1024 * 1024
        ),
    )(tokens, ids, slot[None, :], rw, eg, eu, ed, sg, su, sd)


def solution(mesh):
    placed = (
        P("ep", "tp"),
        P("ep", None),
        P(),
        P("tp", None),
        P("ep", "tp", None),
        P("ep", "tp", None),
        P("ep", None, "tp"),
        P("tp", "ep"),
        P("tp", "ep"),
        P("ep", "tp"),
    )
    return jax.shard_map(
        functools.partial(on_device, mesh.shape["ep"], mesh.shape["tp"]),
        mesh=mesh,
        in_specs=placed,
        out_specs=P("ep", "tp"),
        check_vma=False,
    )
```

time: 421 us -> 110 us (0.26)
  waiting for transfers between devices: 269 us -> 0 us
  Pallas kernels: 0 us -> 99.9 us
  blocking collectives: 74.2 us -> 0 us
  matrix products: 32.8 us -> 0 us
  between operations: 13.3 us -> 0.01 us
  other arithmetic: 11.4 us -> 0 us
  starting transfers between devices: 7.14 us -> 0 us
    all_gather x3 -> x0, waiting for transfers between devices: 191 us -> none  [gathered(): return lax.all_gather(part, axis, axis=dim, tiled=True)]
    pallas_call x0 -> x1, Pallas kernels: none -> 99.9 us  [on_device(): pl.pallas_call(functools.partial(kernel, n_ep, n_tp, chunks), out_shape=j...]
    all_to_all x1 -> x0, blocking collectives: 71.7 us -> none  [on_device(): lax.all_to_all(outgoing, 'ep', split_axis=0, concat_axis=0, tiled=True)]
    all_to_all x1 -> x0, waiting for transfers between devices: 56.7 us -> none  [on_device(): lax.all_to_all(leaving, 'ep', split_axis=0, concat_axis=0, tiled=True)]
    dot_general x7 -> x0, matrix products: 32.8 us -> none  [the longest x1 7.15 us: on_device(): jnp.einsum('erf,efd->erd', hidden, expert_down, preferred_element_type=jn...]
    psum x1 -> x0, waiting for transfers between devices: 19.4 us -> none  [on_device(): pre_gate, pre_up = lax.psum((pre_gate, pre_up), 'tp')]
    select_n x3 -> x0, other arithmetic: 10.2 us -> none  [the longest x1 10.2 us: on_device(): outgoing = jnp.zeros((experts_all * capacity, features), tokens.dtype).at...]
    unnamed x16 -> x5, local copies, waits for them, and re-layouts: 0.79 us -> 9.6 us
  transfers between devices with their start and end apart: 5 -> 0, of which waited for: 5 -> 0; matrix products, arithmetic and copies ran while one was open for 11% -> 0% of each run, Pallas kernels for 0% -> 0%
where the time goes in v1:
time: 110 us; the launch traced here: 109 us
  Pallas kernels  99.9 us (91%)
  local copies, waits for them, and re-layouts  9.6 us (9%)
    pallas_call x1, Pallas kernels, on_device(): pl.pallas_call(functools.partial(kernel, n_ep, n_tp, chunks), out_shape=j...  99.9 us
    unnamed x5, local copies, waits for them, and re-layouts  9.6 us

profile of v1, /device:TPU:0, one launch (start us, length us, event | category | flops | bytes accessed | tf_op | source)
XLA Modules:
  0.0 109.5 jit_solution(3671817674970766779)
XLA Ops:
  0.0 1.4 %copy.11.ids = s32[16,8]{1,0:T(8,128)} copy(s32[16,8]{0,1:T(8,128)} %param.11) | data formatting | bytes 1024 | tf_op args[1]
  1.4 2.1 %copy.12.rw_hbm = bf16[3584,16]{1,0:T(8,128)(2,1)} copy(bf16[3584,16]{0,1:T(8,128)(2,1)} %param.13) | data formatting | bytes 229376 | tf_op args[3]
  3.5 2.3 %copy.13.sg_hbm = bf16[3584,64]{1,0:T(8,128)(2,1)} copy(bf16[3584,64]{0,1:T(8,128)(2,1)} %param.17) | data formatting | bytes 917504 | tf_op args[7]
  5.8 2.3 %copy.14.su_hbm = bf16[3584,64]{1,0:T(8,128)(2,1)} copy(bf16[3584,64]{0,1:T(8,128)(2,1)} %param.18) | data formatting | bytes 917504 | tf_op args[8]
  8.0 99.9 %shard_map.100 = bf16[16,3584]{1,0:T(8,128)(2,1)} custom-call(bf16[16,3584]{1,0:T(8,128)(2,1)} %tokens.1, s32[16,8]{1,0:T(8,128)} %copy.11.ids, s32[1,16]{1,0:T(1,128)} %bitcast.1, bf16[3584,16]{1,0:T(8,128)(2,1)} %copy.12.rw_hbm, bf16[1,3584,1024]{2,1,0:T(8,128)(2,1)} %eg_hbm.1, bf16[1,3584,1024]{2,1,0:T(8,128)(2,1)} %eu_hbm.1, ...), custom_call_target="tpu_custom_call" | custom-call | tf_op jit(solution)/shard_map/pallas_call | solution.py:317
  107.9 1.6 %copy.16 = bf16[16,3584]{1,0:T(8,128)(2,1)} copy(bf16[16,3584]{1,0:T(8,128)(2,1)} %shard_map.100) | data formatting | bytes 229376

commit v2 on v1

--- a/solution.py
+++ b/solution.py
@@ -18,6 +18,10 @@
 
 def dot(a, b):
     return jnp.dot(a, b, preferred_element_type=jnp.float32)
+
+
+def dot_t(a, b):
+    return lax.dot_general(a, b, (((1,), (1,)), ((), ())), preferred_element_type=jnp.float32)
 
 
 def kernel(
@@ -39,9 +43,6 @@
     wg,
     wu,
     wd,
-    rw,
-    sg,
-    su,
     sw,
     sd,
     lg_part,
@@ -77,7 +78,7 @@
     rows, feats = tokens.shape
     experts = slot.shape[1]
     ff_part = wg.shape[2]
-    sff = sg.shape[1]
+    sff = sg_hbm.shape[0]
     width = feats // chunks
 
     def ep_at(d):
@@ -90,9 +91,9 @@
         return ref.at[pl.ds(pl.multiple_of(block * rows, rows), rows), :]
 
     loads = [
-        pltpu.make_async_copy(rw_hbm, rw, w_sem.at[0]),
-        pltpu.make_async_copy(sg_hbm, sg, w_sem.at[1]),
-        pltpu.make_async_copy(su_hbm, su, w_sem.at[2]),
+        pltpu.make_async_copy(rw_hbm, sw.at[2 * sff : 2 * sff + experts, :], w_sem.at[0]),
+        pltpu.make_async_copy(sg_hbm, sw.at[0:sff, :], w_sem.at[1]),
+        pltpu.make_async_copy(su_hbm, sw.at[sff : 2 * sff, :], w_sem.at[2]),
         pltpu.make_async_copy(sd_hbm, sd, w_sem.at[3]),
         pltpu.make_async_copy(ed_hbm.at[0], wd, w_sem.at[4]),
     ]
@@ -123,19 +124,56 @@
 
     pl.semaphore_wait(barrier, n_ep + n_tp - 2)
 
-    def token_copy(src, to):
+    near = 1 + lax.rem(tp, 2)
+    far = 3 - near
+    line = n_ep // 4
+    level = ep // 4
+    near_bit, far_bit = lax.rem(ep // near, 2), lax.rem(ep // far, 2)
+    near_peer = ep + near * (1 - 2 * near_bit)
+    far_peer = ep + far * (1 - 2 * far_bit)
+
+    def token_copy(way, src, to, src_ref=None):
         return pltpu.make_async_remote_copy(
-            src_ref=tokens,
+            src_ref=row_block(x, src) if src_ref is None else src_ref,
             dst_ref=row_block(x, src),
-            send_sem=x_send.at[to],
+            send_sem=x_send.at[way, src],
             recv_sem=x_recv.at[src],
             device_id={"ep": to},
             device_id_type=MESH,
         )
 
-    @pl.loop(1, n_ep)
-    def _(d):
-        token_copy(ep, ep_at(d)).start()
+    def pass_on(src, up, down, src_ref=None):
+        @pl.when(up)
+        def _():
+            token_copy(0, src, lax.rem(ep + 4, n_ep), src_ref).start()
+
+        @pl.when(down)
+        def _():
+            token_copy(1, src, lax.rem(ep + n_ep - 4, n_ep), src_ref).start()
+
+        token_copy(2, src, far_peer, src_ref).start()
+
+    can_up, can_down = level < line - 1, level > 0
+    token_copy(3, ep, near_peer, tokens).start()
+    pass_on(ep, can_up, can_down, tokens)
+
+    token_copy(3, near_peer, near_peer).wait_recv()
+    pass_on(near_peer, can_up, can_down)
+
+    @pl.loop(1, line)
+    def _(far_off):
+        for side in (ep, near_peer):
+            below, above = side - 4 * far_off, side + 4 * far_off
+
+            @pl.when(level >= far_off)
+            def _():
+                token_copy(0, below, ep).wait_recv()
+                pass_on(below, can_up, False)
+
+            @pl.when(level + far_off < line)
+            def _():
+                token_copy(1, above, ep).wait_recv()
+                pass_on(above, False, can_down)
 
     def to_tp(src_ref, in_ref, send, recv, slot_in, to):
         return pltpu.make_async_remote_copy(
@@ -148,17 +186,12 @@
         )
 
     loads[0].wait()
-    lg_part[...] = dot(tokens[...], rw[...])
+    lg_part[...] = dot_t(tokens[...], sw[2 * sff : 2 * sff + experts, :])
     lg_in[tp] = lg_part[...]
 
     @pl.loop(1, n_tp)
     def _(d):
         to_tp(lg_part, lg_in, lg_send, lg_recv, tp, tp_at(d)).start()
-
-    loads[1].wait()
-    loads[2].wait()
-    sw[:, 0:sff] = sg[...]
-    sw[:, sff : 2 * sff] = su[...]
 
     @pl.loop(1, n_tp)
     def _(d):
@@ -167,10 +200,14 @@
     logits = lg_in[0]
     for j in range(1, n_tp):
         logits = logits + lg_in[j]
-    expert_iota = lax.broadcasted_iota(jnp.int32, (rows, experts), 1)
-    mask = jnp.zeros((rows, experts), jnp.float32)
-    for k in range(ids.shape[1]):
-        mask = mask + jnp.where(ids[:, k : k + 1] == expert_iota, 1.0, 0.0)
+    turned_iota = lax.broadcasted_iota(jnp.int32, (experts, rows), 0)
+    turned = jnp.zeros((experts, rows), jnp.float32)
+    for k in range(ids.shape[0]):
+        turned = turned + jnp.where(ids[k : k + 1, :] == turned_iota, 1.0, 0.0)
+    row_iota = lax.broadcasted_iota(jnp.int32, (rows, rows), 0)
+    same = row_iota == lax.broadcasted_iota(jnp.int32, (rows, rows), 1)
+    eye = jnp.where(same, 1.0, 0.0).astype(jnp.bfloat16)
+    mask = dot_t(eye, turned.astype(jnp.bfloat16))
     picked = mask * (1.0 / (1.0 + jnp.exp(-logits)))
     gates[...] = picked / jnp.sum(picked, axis=1, keepdims=True) * route_scale
     gates_in[pl.ds(pl.multiple_of(ep * rows, rows), rows), :] = gates[...]
@@ -191,9 +228,22 @@
 
     own.wait()
 
-    @pl.loop(1, n_ep)
-    def _(d):
-        token_copy(ep_at(d), ep_at(d)).wait()
+    @pl.loop(0, line)
+    def _(at):
+        for side in (ep, near_peer):
+            mine_there = lax.rem(side, 4) + 4 * at
+            token_copy(2, mine_there + far * (1 - 2 * far_bit), ep).wait_recv()
+            token_copy(2, mine_there, far_peer).wait_send()
+
+            @pl.when(can_up & (at <= level))
+            def _():
+                token_copy(0, mine_there, ep).wait_send()
+
+            @pl.when(can_down & (at >= level))
+            def _():
+                token_copy(1, mine_there, ep).wait_send()
+
+    token_copy(3, ep, near_peer).wait_send()
 
     def gate_up(j):
         piece_load(eg_hbm, wg, j, 5).wait()
@@ -207,7 +257,9 @@
         gate_up(j)
         to_tp(part.at[j], part_in, pa_send, pa_recv, tp, j).start()
 
-    sh_part[...] = dot(x[...], sw[...])
+    loads[1].wait()
+    loads[2].wait()
+    sh_part[...] = dot_t(x[...], sw[0 : 2 * sff, :])
 
     @pl.loop(1, n_tp)
     def _(d):
@@ -306,6 +358,7 @@
     experts = slot.shape[0]
     ff = eg.shape[2]
     sff = sg.shape[1]
+    assert n_ep % 4 == 0
     everyone = rows * n_ep
     ff_part = ff // n_tp
     chunks = math.gcd(feats // 128, 4)
@@ -324,10 +377,7 @@
             pltpu.VMEM((n_tp, feats, ff_part), bf),
             pltpu.VMEM((n_tp, feats, ff_part), bf),
             pltpu.VMEM((ff, feats), bf),
-            pltpu.VMEM((feats, experts), bf),
-            pltpu.VMEM((feats, sff), bf),
-            pltpu.VMEM((feats, sff), bf),
-            pltpu.VMEM((feats, 2 * sff), bf),
+            pltpu.VMEM((2 * sff + experts, feats), bf),
             pltpu.VMEM((sff, feats), bf),
             pltpu.VMEM((rows, experts), f32),
             pltpu.VMEM((n_tp, rows, experts), f32),
@@ -343,7 +393,7 @@
             pltpu.VMEM((chunks, everyone, width), bf),
             dma((5 + 2 * n_tp,)),
             dma((1,)),
-            dma((n_ep,)),
+            dma((4, n_ep)),
             dma((n_ep,)),
             dma((n_tp,)),
             dma((n_tp,)),
@@ -361,7 +411,7 @@
         compiler_params=pltpu.CompilerParams(
             collective_id=0, has_side_effects=True, vmem_limit_bytes=63 * 1024 * 1024
         ),
-    )(tokens, ids, slot[None, :], rw, eg, eu, ed, sg, su, sd)
+    )(tokens, ids.T, slot[None, :], rw.T, eg, eu, ed, sg.T, su.T, sd)
 
 
 def solution(mesh):

time: 110 us -> 77.1 us (0.70)
  Pallas kernels: 99.9 us -> 75.4 us
  local copies, waits for them, and re-layouts: 9.6 us -> 1.55 us
    pallas_call x1, Pallas kernels: 99.9 us -> 75.4 us  [on_device(): pl.pallas_call(functools.partial(kernel, n_ep, n_tp, chunks), out_shape=j...]
    unnamed x5 -> x1, local copies, waits for them, and re-layouts: 9.6 us -> 1.55 us
where the time goes in v2:
time: 77.1 us; the launch traced here: 77 us
  Pallas kernels  75.4 us (98%)
  local copies, waits for them, and re-layouts  1.55 us (2%)
    pallas_call x1, Pallas kernels, on_device(): pl.pallas_call(functools.partial(kernel, n_ep, n_tp, chunks), out_shape=j...  75.4 us
    unnamed x1, local copies, waits for them, and re-layouts  1.55 us

profile of v2, /device:TPU:0, one launch (start us, length us, event | category | flops | bytes accessed | tf_op | source)
XLA Modules:
  0.0 77.0 jit_solution(3847179048353568173)
XLA Ops:
  0.0 75.4 %shard_map.100 = bf16[16,3584]{1,0:T(8,128)(2,1)} custom-call(bf16[16,3584]{1,0:T(8,128)(2,1)} %tokens.1, s32[8,16]{1,0:T(8,128)} %bitcast.8, s32[1,16]{1,0:T(1,128)} %bitcast.9, bf16[16,3584]{1,0:T(8,128)(2,1)} %bitcast.7, bf16[1,3584,1024]{2,1,0:T(8,128)(2,1)} %eg_hbm.1, bf16[1,3584,1024]{2,1,0:T(8,128)(2,1)} %eu_hbm.1, bf16[1,1024,3584]{2,1,0:T(8,128)(2,1)} %ed_hbm.1, ...), custom_call_target="tpu_custom_call" | custom-call | tf_op jit(solution)/shard_map/pallas_call | solution.py:370
  75.4 1.6 %copy.12 = bf16[16,3584]{1,0:T(8,128)(2,1)} copy(bf16[16,3584]{1,0:T(8,128)(2,1)} %shard_map.100) | data formatting | bytes 229376

commit v3 on v2

--- a/solution.py
+++ b/solution.py
@@ -55,8 +55,14 @@
     sh_in,
     hid,
     hid_in,
-    leave,
-    arrive,
+    whole,
+    keep,
+    leave_far,
+    come_far,
+    leave_line,
+    come_line,
+    leave_near,
+    come_near,
     w_sem,
     own_sem,
     x_send,
@@ -71,8 +77,12 @@
     sh_recv,
     hi_send,
     hi_recv,
-    le_send,
-    le_recv,
+    far_send,
+    far_recv,
+    line_send,
+    line_recv,
+    near_send,
+    near_recv,
 ):
     ep, tp = lax.axis_index("ep"), lax.axis_index("tp")
     rows, feats = tokens.shape
@@ -310,15 +320,42 @@
         j = tp_at(d)
         to_tp(hid, hid_in, hi_send, hi_recv, j, j).wait()
 
-    def leave_copy(chunk, src, to):
+    half = 2 * line
+    pair = 2 * rows
+    here = pl.ds(pl.multiple_of(level * pair, pair), pair)
+
+    def far_copy(chunk):
         return pltpu.make_async_remote_copy(
-            src_ref=row_block(leave.at[chunk], to),
-            dst_ref=row_block(arrive.at[chunk], src),
-            send_sem=le_send.at[chunk, to],
-            recv_sem=le_recv.at[chunk, src],
-            device_id={"ep": to},
+            src_ref=leave_far.at[chunk],
+            dst_ref=come_far.at[chunk],
+            send_sem=far_send.at[chunk],
+            recv_sem=far_recv.at[chunk],
+            device_id={"ep": far_peer},
             device_id_type=MESH,
         )
+
+    def line_copy(chunk, src, to):
+        return pltpu.make_async_remote_copy(
+            src_ref=leave_line.at[chunk, pl.ds(pl.multiple_of(to * pair, pair), pair), :],
+            dst_ref=come_line.at[chunk, pl.ds(pl.multiple_of(src * pair, pair), pair), :],
+            send_sem=line_send.at[chunk, to],
+            recv_sem=line_recv.at[chunk, src],
+            device_id={"ep": lax.rem(ep, 4) + 4 * to},
+            device_id_type=MESH,
+        )
+
+    def near_copy(chunk):
+        return pltpu.make_async_remote_copy(
+            src_ref=leave_near.at[chunk],
+            dst_ref=come_near.at[chunk],
+            send_sem=near_send.at[chunk],
+            recv_sem=near_recv.at[chunk],
+            device_id={"ep": near_peer},
+            device_id_type=MESH,
+        )
+
+    def level_at(d):
+        return lax.rem(level + d, line)
 
     @pl.loop(0, chunks)
     def _(chunk):
@@ -327,29 +364,50 @@
         for j in range(1, n_tp):
             total = total + dot(hid_in[j], wd[j * ff_part : (j + 1) * ff_part, cols])
         given = total.astype(jnp.bfloat16).astype(jnp.float32) * column
-        given = given + dot(sh_hid, sd[:, cols])
-        leave[chunk] = given.astype(jnp.bfloat16)
-
-        @pl.loop(1, n_ep)
-        def _(d):
-            leave_copy(chunk, ep, ep_at(d)).start()
+        whole[...] = given + dot(sh_hid, sd[:, cols])
+
+        @pl.loop(0, half)
+        def _(k):
+            owner = 4 * (k // 2) + near * lax.rem(k, 2)
+            at = pl.ds(pl.multiple_of(k * rows, rows), rows)
+            kept = pl.multiple_of((owner + far * far_bit) * rows, rows)
+            sent = pl.multiple_of((owner + far * (1 - far_bit)) * rows, rows)
+            keep[chunk, at, :] = whole[pl.ds(kept, rows), :]
+            leave_far[chunk, at, :] = whole[pl.ds(sent, rows), :].astype(jnp.bfloat16)
+
+        far_copy(chunk).start()
 
     @pl.loop(0, chunks)
     def _(chunk):
-        cols = pl.ds(pl.multiple_of(chunk * width, width), width)
-        here = pl.ds(pl.multiple_of(ep * rows, rows), rows)
-        arrive[chunk, here, :] = leave[chunk, here, :]
-
-        @pl.loop(1, n_ep)
+        far_copy(chunk).wait()
+        both = keep[chunk] + come_far[chunk].astype(jnp.float32)
+        keep[chunk] = both
+        leave_line[chunk] = both.astype(jnp.bfloat16)
+
+        @pl.loop(1, line)
         def _(d):
-            leave_copy(chunk, ep_at(d), ep_at(d)).wait()
-
-        def add(src, total):
-            block = arrive[chunk, pl.ds(pl.multiple_of(src * rows, rows), rows), :]
-            return total + block.astype(jnp.float32)
-
-        total = lax.fori_loop(0, n_ep, add, jnp.zeros((rows, width), jnp.float32))
-        out[:, cols] = total.astype(jnp.bfloat16)
+            line_copy(chunk, level, level_at(d)).start()
+
+    @pl.loop(0, chunks)
+    def _(chunk):
+        @pl.loop(1, line)
+        def _(d):
+            line_copy(chunk, level_at(d), level_at(d)).wait()
+
+        def add(d, total):
+            src = pl.multiple_of(level_at(d) * pair, pair)
+            return total + come_line[chunk, pl.ds(src, pair), :].astype(jnp.float32)
+
+        keep[chunk, here, :] = lax.fori_loop(1, line, add, keep[chunk, here, :])
+        other = pl.multiple_of(level * pair + (1 - near_bit) * rows, rows)
+        leave_near[chunk] = keep[chunk, pl.ds(other, rows), :]
+        near_copy(chunk).start()
+
+    for chunk in range(chunks):
+        near_copy(chunk).wait()
+        mine_at = pl.multiple_of(level * pair + near_bit * rows, rows)
+        done = keep[chunk, pl.ds(mine_at, rows), :] + come_near[chunk]
+        out[:, chunk * width : (chunk + 1) * width] = done.astype(jnp.bfloat16)
 
 
 def on_device(n_ep, n_tp, *args):
@@ -361,7 +419,7 @@
     assert n_ep % 4 == 0
     everyone = rows * n_ep
     ff_part = ff // n_tp
-    chunks = math.gcd(feats // 128, 4)
+    chunks = math.gcd(feats // 128, 7)
     width = feats // chunks
     bf, f32 = jnp.bfloat16, jnp.float32
     dma = pltpu.SemaphoreType.DMA
@@ -389,8 +447,14 @@
             pltpu.VMEM((n_tp, everyone, 2 * sff), f32),
             pltpu.VMEM((everyone, ff_part), bf),
             pltpu.VMEM((n_tp, everyone, ff_part), bf),
-            pltpu.VMEM((chunks, everyone, width), bf),
-            pltpu.VMEM((chunks, everyone, width), bf),
+            pltpu.VMEM((everyone, width), f32),
+            pltpu.VMEM((chunks, everyone // 2, width), f32),
+            pltpu.VMEM((chunks, everyone // 2, width), bf),
+            pltpu.VMEM((chunks, everyone // 2, width), bf),
+            pltpu.VMEM((chunks, everyone // 2, width), bf),
+            pltpu.VMEM((chunks, everyone // 2, width), bf),
+            pltpu.VMEM((chunks, rows, width), f32),
+            pltpu.VMEM((chunks, rows, width), f32),
             dma((5 + 2 * n_tp,)),
             dma((1,)),
             dma((4, n_ep)),
@@ -405,8 +469,12 @@
             dma((n_tp,)),
             dma((n_tp,)),
             dma((n_tp,)),
-            dma((chunks, n_ep)),
-            dma((chunks, n_ep)),
+            dma((chunks,)),
+            dma((chunks,)),
+            dma((chunks, n_ep // 4)),
+            dma((chunks, n_ep // 4)),
+            dma((chunks,)),
+            dma((chunks,)),
         ],
         compiler_params=pltpu.CompilerParams(
             collective_id=0, has_side_effects=True, vmem_limit_bytes=63 * 1024 * 1024

time: 77.1 us -> 65 us (0.84)
  Pallas kernels: 75.4 us -> 63.3 us
    pallas_call x1, Pallas kernels: 75.4 us -> 63.3 us  [on_device(): pl.pallas_call(functools.partial(kernel, n_ep, n_tp, chunks), out_shape=j...]
where the time goes in v3:
time: 65 us; the launch traced here: 64.8 us
  Pallas kernels  63.3 us (97%)
  local copies, waits for them, and re-layouts  1.55 us (2%)
    pallas_call x1, Pallas kernels, on_device(): pl.pallas_call(functools.partial(kernel, n_ep, n_tp, chunks), out_shape=j...  63.3 us
    unnamed x1, local copies, waits for them, and re-layouts  1.55 us

profile of v3, /device:TPU:0, one launch (start us, length us, event | category | flops | bytes accessed | tf_op | source)
XLA Modules:
  0.0 64.8 jit_solution(12988590816533576834)
XLA Ops:
  0.0 63.3 %shard_map.100 = bf16[16,3584]{1,0:T(8,128)(2,1)} custom-call(bf16[16,3584]{1,0:T(8,128)(2,1)} %tokens.1, s32[8,16]{1,0:T(8,128)} %bitcast.8, s32[1,16]{1,0:T(1,128)} %bitcast.9, bf16[16,3584]{1,0:T(8,128)(2,1)} %bitcast.7, bf16[1,3584,1024]{2,1,0:T(8,128)(2,1)} %eg_hbm.1, bf16[1,3584,1024]{2,1,0:T(8,128)(2,1)} %eu_hbm.1, bf16[1,1024,3584]{2,1,0:T(8,128)(2,1)} %ed_hbm.1, ...), custom_call_target="tpu_custom_call" | custom-call | tf_op jit(solution)/shard_map/pallas_call | solution.py:428
  63.3 1.6 %copy.12 = bf16[16,3584]{1,0:T(8,128)(2,1)} copy(bf16[16,3584]{1,0:T(8,128)(2,1)} %shard_map.100) | data formatting | bytes 229376
